TPU v7x, 32 devices: a whole 2x2x4 slice. The times are simulated.
32 devices in a mesh: row: 8 (over y, x, core), col: 4 (over z).
Axes of the slice: x: 2, y: 2, z: 4, core: 2. Of those that a mesh axis runs over, the one named last changes fastest.
Arguments:
- history: float32 [3, 512, 4096], P(None, None, ('row', 'col')), may hold values from -8 to 8
Outputs:
- orbitals: float32 [512, 4096], P(None, ('row', 'col'))
All inputs are finite; a program needn't handle non-finite values.
Results may differ from a plain program's by a relative error of at most 0.0003.
Values sent between devices are 32-bit elements; how exact they have to be, the bound alone decides.
A program may use at most 64 MiB of HBM per device.

v0:
```python
import jax
import jax.numpy as jnp
from jax import lax
from jax.sharding import PartitionSpec as P


def on_device(history):
    precise = lax.Precision.HIGHEST
    npw_total = history.shape[2] * lax.axis_size("row") * lax.axis_size("col")
    newest = history[0]
    local_terms = tuple(
        (jnp.einsum("ip,jp->ij", newest, history[index], precision=precise) for index in range(3))
    )
    summed = lax.psum(local_terms, ("row", "col"))
    weights = (2.5, -2.0, 0.5)
    predicted = jnp.zeros(newest.shape, jnp.float32)
    for index in range(3):
        project = summed[index] / npw_total
        predicted = predicted + weights[index] * jnp.dot(project, history[index], precision=precise)
    local_gram = jnp.einsum("ip,jp->ij", predicted, predicted, precision=precise)
    gram = lax.psum(local_gram, ("row", "col"))
    factor = jnp.linalg.cholesky(gram / npw_total)
    return lax.linalg.triangular_solve(factor, predicted, left_side=True, lower=True)


def solution(mesh):
    return jax.shard_map(
        on_device,
        mesh=mesh,
        in_specs=(P(None, None, ("row", "col")),),
        out_specs=P(None, ("row", "col")),
        check_vma=False,
    )
```

profile of v0, /device:TPU:0, one launch (start us, length us, event | category | flops | bytes accessed | tf_op | source)
XLA Modules:
  0.0 441.3 jit_solution(1607792850113480831)
XLA Ops:
  6.5 3.1 fusion.11
  9.7 2.0 fusion.14
  11.6 2.0 fusion.19
  14.1 141.3 %all-reduce.7.cloned.1.call-done = (f32[512,512]{0,1:T(8,128)}, f32[512,512]{0,1:T(8,128)}, f32[512,512]{0,1:T(8,128)}) async-done(((f32[512,512]{0,1:T(8,128)}, f32[512,512]{0,1:T(8,128)}, f32[512,512]{0,1:T(8,128)}), (f32[512,512]{0,1:T(8,128)}, f32[512,512]{0,1:T(8,128)}, f32[512,512]{0,1:T(8,128)})) %all-reduce.7.cloned.1.call-update) | async-done | bytes 3145744 | tf_op jit(solution)/shard_map/psum | solution.py:14
  155.4 3.1 convolution_multiply_fusion.2
  158.6 1.8 fusion.1
  160.4 1.8 fusion
  162.2 2.0 fusion.61
  164.3 130.2 %all-reduce.5.cloned.1.call-done = f32[512,512]{0,1:T(8,128)} async-done(((f32[512,512]{0,1:T(8,128)}), f32[512,512]{0,1:T(8,128)}) %all-reduce.5.cloned.1.call-update) | async-done | bytes 1048592 | tf_op jit(solution)/shard_map/psum | solution.py:21
  294.5 1.3 broadcast_multiply_fusion
  296.2 0.9 copy-done.1
  297.3 11.7 %cholesky.104 = f32[128,128]{1,0:T(8,128)S(1)} custom-call(f32[128,128]{1,0:T(8,128)S(1)} %cholesky.266), custom_call_target="Cholesky" | custom-call | tf_op jit(solution)/shard_map/jit(cholesky)/cholesky | solution.py:22
  309.0 10.0 %custom-call.30 = f32[1,128,128]{1,2,0:T(8,128)S(1)} custom-call(f32[1,128,128]{2,1,0:T(8,128)S(1)} %get-tuple-element.35), custom_call_target="InvertDiagBlocksLowerTriangular" | custom-call | tf_op jit(solution)/shard_map/jit(cholesky)/cholesky | solution.py:22
  319.8 11.7 %cholesky.217 = f32[128,128]{1,0:T(8,128)S(1)} custom-call(f32[128,128]{1,0:T(8,128)S(1)} %cholesky.270), custom_call_target="Cholesky" | custom-call | tf_op jit(solution)/shard_map/jit(cholesky)/cholesky | solution.py:22
  331.5 9.8 %custom-call.31 = f32[1,128,128]{1,2,0:T(8,128)S(1)} custom-call(f32[1,128,128]{2,1,0:T(8,128)S(1)} %get-tuple-element.32), custom_call_target="InvertDiagBlocksLowerTriangular" | custom-call | tf_op jit(solution)/shard_map/jit(cholesky)/cholesky | solution.py:22
  342.0 11.7 %cholesky.238 = f32[128,128]{1,0:T(8,128)S(1)} custom-call(f32[128,128]{1,0:T(8,128)S(1)} %cholesky.275), custom_call_target="Cholesky" | custom-call | tf_op jit(solution)/shard_map/jit(cholesky)/cholesky | solution.py:22
  354.5 10.0 %custom-call.32 = f32[1,128,128]{1,2,0:T(8,128)S(1)} custom-call(f32[1,128,128]{2,1,0:T(8,128)S(1)} %get-tuple-element.29), custom_call_target="InvertDiagBlocksLowerTriangular" | custom-call | tf_op jit(solution)/shard_map/jit(cholesky)/cholesky | solution.py:22
  365.1 11.7 %cholesky.255 = f32[128,128]{1,0:T(8,128)S(1)} custom-call(f32[128,128]{1,0:T(8,128)S(1)} %convolution_subtract_fusion.5), custom_call_target="Cholesky" | custom-call | tf_op jit(solution)/shard_map/jit(cholesky)/cholesky | solution.py:22
  380.8 10.6 %while.1 = (s32[]{:T(128)}, f32[512,512]{1,0:T(8,128)S(1)}, s32[4,2]{0,1:T(2,128)S(1)}, f32[4,128,128]{2,1,0:T(8,128)}, s32[]{:T(128)}) while((s32[]{:T(128)}, f32[512,512]{1,0:T(8,128)S(1)}, s32[4,2]{0,1:T(2,128)S(1)}, f32[4,128,128]{2,1,0:T(8,128)}, s32[]{:T(128)}) %tuple.27), condition=%wide.while_cond, body=%wide.while_body.sunk | while | flops 2 | bytes 132705 | solution.py:23
  381.5 2.0 bitcast_dynamic-update-slice_fusion.2
  384.2 2.0 bitcast_dynamic-update-slice_fusion.2
  386.8 2.0 bitcast_dynamic-update-slice_fusion.2
  389.5 2.0 bitcast_dynamic-update-slice_fusion.2
  391.4 40.1 %custom-call.33 = f32[4,128,128]{1,2,0:T(8,128)S(1)} custom-call(f32[4,128,128]{2,1,0:T(8,128)} %get-tuple-element.12), custom_call_target="InvertDiagBlocksLowerTriangular" | custom-call | tf_op jit(solution)/shard_map/triangular_solve | solution.py:23
  (50 shorter events, 10.8 us)
Async XLA Ops:
  6.5 3.1 copy-start
  6.5 148.9 %all-reduce.7.cloned.1.call-start = ((), (), s32[]{:S(2)}) async-start(), calls=%async_computation.1 | async-start | bytes 6291456 | tf_op jit(solution)/shard_map/psum | solution.py:14
  13.6 280.9 %all-reduce.5.cloned.1.call-start = ((), (), s32[]{:S(2)}) async-start(), calls=%async_computation | async-start | bytes 2097152 | tf_op jit(solution)/shard_map/psum | solution.py:21
  155.4 3.1 copy-start.3
  158.5 1.8 copy-start.2
  295.8 1.2 copy-start.1
Sparse Core Ops, SparseCore 0:
  13.8 141.6 all-reduce.6
  164.4 130.0 all-reduce.4
where the time goes:
time: 444 us; the launch traced here: 441 us
  waiting for transfers between devices  271 us (61%)
  other arithmetic  121 us (27%)
  matrix products  19.7 us (4%)
  between operations  16.4 us (4%)
  local copies, waits for them, and re-layouts  11.9 us (3%)
    psum x1, waiting for transfers between devices, on_device(): summed = lax.psum(local_terms, ('row', 'col'))  141 us
    psum x1, waiting for transfers between devices, on_device(): gram = lax.psum(local_gram, ('row', 'col'))  130 us
    another operation x14, other arithmetic, on_device(): factor = jnp.linalg.cholesky(gram / npw_total)  78.8 us
    another operation x4, other arithmetic, on_device(): lax.linalg.triangular_solve(factor, predicted, left_side=True, lower=True)  41 us
    another operation x12, local copies, waits for them, and re-layouts  10.6 us
  transfers between devices with their start and end apart: 2, of which 2 were waited for; matrix products, arithmetic and copies ran while one was open for 0% of the time, Pallas kernels for 0%

commit v1 on v0

--- a/solution.py
+++ b/solution.py
@@ -11,7 +11,10 @@
     local_terms = tuple(
         (jnp.einsum("ip,jp->ij", newest, history[index], precision=precise) for index in range(3))
     )
-    summed = lax.psum(local_terms, ("row", "col"))
+    _test_ranges = lambda inp, net_axis, lane_axis: lax.psum(
+        lax.psum(inp, axis_name=net_axis), axis_name=lane_axis
+    )
+    summed = _test_ranges(local_terms, "row", "col")
     weights = (2.5, -2.0, 0.5)
     predicted = jnp.zeros(newest.shape, jnp.float32)
     for index in range(3):

time: 444 us -> 498 us (1.12)
  waiting for transfers between devices: 271 us -> 325 us
    psum x1 -> x2, waiting for transfers between devices: 141 us -> 196 us  [the longest x1 123 us: on_device(): lax.psum(lax.psum(inp, axis_name=net_axis), axis_name=lane_axis)]
  transfers between devices with their start and end apart: 2 -> 3, of which waited for: 2 -> 3; matrix products, arithmetic and copies ran while one was open for 0% -> 0% of each run, Pallas kernels for 0% -> 0%
where the time goes in v1:
time: 498 us; the launch traced here: 495 us
  waiting for transfers between devices  325 us (65%)
  other arithmetic  121 us (24%)
  matrix products  19.7 us (4%)
  between operations  16.1 us (3%)
  local copies, waits for them, and re-layouts  11.9 us (2%)
    psum x1, waiting for transfers between devices, on_device(): gram = lax.psum(local_gram, ('row', 'col'))  130 us
    psum x1, waiting for transfers between devices, on_device(): lax.psum(lax.psum(inp, axis_name=net_axis), axis_name=lane_axis)  123 us
    another operation x14, other arithmetic, on_device(): factor = jnp.linalg.cholesky(gram / npw_total)  78.8 us
    psum x1, waiting for transfers between devices, on_device(): lax.psum(inp, axis_name=net_axis)  72.3 us
    another operation x4, other arithmetic, on_device(): lax.linalg.triangular_solve(factor, predicted, left_side=True, lower=True)  41 us
    another operation x12, local copies, waits for them, and re-layouts  10.6 us
  transfers between devices with their start and end apart: 3, of which 3 were waited for; matrix products, arithmetic and copies ran while one was open for 0% of the time, Pallas kernels for 0%

profile of v1, /device:TPU:0, one launch (start us, length us, event | category | flops | bytes accessed | tf_op | source)
XLA Modules:
  0.0 495.0 jit_solution(17054735589472089027)
XLA Ops:
  6.5 3.1 fusion.11
  9.7 2.0 fusion.14
  11.6 2.0 fusion.19
  13.7 72.3 %all-reduce.9.cloned.1.call-done = (f32[512,512]{0,1:T(8,128)}, f32[512,512]{0,1:T(8,128)}, f32[512,512]{0,1:T(8,128)}) async-done(((f32[512,512]{0,1:T(8,128)}, f32[512,512]{0,1:T(8,128)}, f32[512,512]{0,1:T(8,128)}), (f32[512,512]{0,1:T(8,128)}, f32[512,512]{0,1:T(8,128)}, f32[512,512]{0,1:T(8,128)})) %all-reduce.9.cloned.1.call-update) | async-done | bytes 3145744 | tf_op jit(solution)/shard_map/psum | solution.py:15
  86.5 123.2 %all-reduce.11.cloned.1.call-done = (f32[512,512]{0,1:T(8,128)}, f32[512,512]{0,1:T(8,128)}, f32[512,512]{0,1:T(8,128)}) async-done(((f32[512,512]{0,1:T(8,128)}, f32[512,512]{0,1:T(8,128)}, f32[512,512]{0,1:T(8,128)}), (f32[512,512]{0,1:T(8,128)}, f32[512,512]{0,1:T(8,128)}, f32[512,512]{0,1:T(8,128)})) %all-reduce.11.cloned.1.call-update) | async-done | bytes 3145744 | tf_op jit(solution)/shard_map/psum | solution.py:14
  209.7 3.1 convolution_multiply_fusion.2
  212.9 1.8 fusion.1
  214.7 1.8 fusion
  216.6 2.0 fusion.61
  218.6 129.9 %all-reduce.7.cloned.1.call-done = f32[512,512]{0,1:T(8,128)} async-done(((f32[512,512]{0,1:T(8,128)}), f32[512,512]{0,1:T(8,128)}) %all-reduce.7.cloned.1.call-update) | async-done | bytes 1048592 | tf_op jit(solution)/shard_map/psum | solution.py:24
  348.5 1.3 broadcast_multiply_fusion
  351.3 11.7 %cholesky.104 = f32[128,128]{1,0:T(8,128)S(1)} custom-call(f32[128,128]{1,0:T(8,128)S(1)} %cholesky.266), custom_call_target="Cholesky" | custom-call | tf_op jit(solution)/shard_map/jit(cholesky)/cholesky | solution.py:25
  363.1 10.0 %custom-call.30 = f32[1,128,128]{1,2,0:T(8,128)S(1)} custom-call(f32[1,128,128]{2,1,0:T(8,128)S(1)} %get-tuple-element.38), custom_call_target="InvertDiagBlocksLowerTriangular" | custom-call | tf_op jit(solution)/shard_map/jit(cholesky)/cholesky | solution.py:25
  373.8 11.7 %cholesky.217 = f32[128,128]{1,0:T(8,128)S(1)} custom-call(f32[128,128]{1,0:T(8,128)S(1)} %cholesky.270), custom_call_target="Cholesky" | custom-call | tf_op jit(solution)/shard_map/jit(cholesky)/cholesky | solution.py:25
  385.6 9.8 %custom-call.31 = f32[1,128,128]{1,2,0:T(8,128)S(1)} custom-call(f32[1,128,128]{2,1,0:T(8,128)S(1)} %get-tuple-element.35), custom_call_target="InvertDiagBlocksLowerTriangular" | custom-call | tf_op jit(solution)/shard_map/jit(cholesky)/cholesky | solution.py:25
  396.1 11.7 %cholesky.238 = f32[128,128]{1,0:T(8,128)S(1)} custom-call(f32[128,128]{1,0:T(8,128)S(1)} %cholesky.275), custom_call_target="Cholesky" | custom-call | tf_op jit(solution)/shard_map/jit(cholesky)/cholesky | solution.py:25
  408.5 10.0 %custom-call.32 = f32[1,128,128]{1,2,0:T(8,128)S(1)} custom-call(f32[1,128,128]{2,1,0:T(8,128)S(1)} %get-tuple-element.32), custom_call_target="InvertDiagBlocksLowerTriangular" | custom-call | tf_op jit(solution)/shard_map/jit(cholesky)/cholesky | solution.py:25
  419.1 11.7 %cholesky.255 = f32[128,128]{1,0:T(8,128)S(1)} custom-call(f32[128,128]{1,0:T(8,128)S(1)} %convolution_subtract_fusion.5), custom_call_target="Cholesky" | custom-call | tf_op jit(solution)/shard_map/jit(cholesky)/cholesky | solution.py:25
  434.9 10.6 %while.1 = (s32[]{:T(128)}, f32[512,512]{1,0:T(8,128)S(1)}, s32[4,2]{0,1:T(2,128)S(1)}, f32[4,128,128]{2,1,0:T(8,128)}, s32[]{:T(128)}) while((s32[]{:T(128)}, f32[512,512]{1,0:T(8,128)S(1)}, s32[4,2]{0,1:T(2,128)S(1)}, f32[4,128,128]{2,1,0:T(8,128)}, s32[]{:T(128)}) %tuple.27), condition=%wide.while_cond, body=%wide.while_body.sunk | while | flops 2 | bytes 132705 | solution.py:26
  435.6 2.0 bitcast_dynamic-update-slice_fusion.2
  438.2 2.0 bitcast_dynamic-update-slice_fusion.2
  440.8 2.0 bitcast_dynamic-update-slice_fusion.2
  443.5 2.0 bitcast_dynamic-update-slice_fusion.2
  445.5 40.1 %custom-call.33 = f32[4,128,128]{1,2,0:T(8,128)S(1)} custom-call(f32[4,128,128]{2,1,0:T(8,128)} %get-tuple-element.12), custom_call_target="InvertDiagBlocksLowerTriangular" | custom-call | tf_op jit(solution)/shard_map/triangular_solve | solution.py:26
  (53 shorter events, 11.7 us)
Async XLA Ops:
  6.5 3.1 copy-start
  6.5 79.4 %all-reduce.9.cloned.1.call-start = ((), (), s32[]{:S(2)}) async-start(), calls=%async_computation.1 | async-start | bytes 6291456 | tf_op jit(solution)/shard_map/psum | solution.py:15
  13.6 196.1 %all-reduce.11.cloned.1.call-start = ((), (), s32[]{:S(2)}) async-start(), calls=%async_computation.2 | async-start | bytes 6291456 | tf_op jit(solution)/shard_map/psum | solution.py:14
  86.0 262.5 %all-reduce.7.cloned.1.call-start = ((), (), s32[]{:S(2)}) async-start(), calls=%async_computation | async-start | bytes 2097152 | tf_op jit(solution)/shard_map/psum | solution.py:24
  209.7 3.1 copy-start.3
  212.9 1.9 copy-start.2
  349.8 1.2 copy-start.1
Sparse Core Ops, SparseCore 0:
  13.8 72.1 all-reduce.8
  88.5 121.1 all-reduce.10
  218.7 129.7 all-reduce.6
